TPU v7x, 128 devices: a whole 4x4x4 slice. The times are simulated.
128 devices in a mesh: gx: 4 (over z), gy: 4 (over y), gz: 8 (over x, core).
Axes of the slice: x: 4, y: 4, z: 4, core: 2. Of those that a mesh axis runs over, the one named last changes fastest.
Arguments:
- interact: bfloat16 [16, 32768, 512], P(None, ('gx', 'gy', 'gz')), may hold values from -6 to 6
- weight_one: bfloat16 [512, 1024], replicated, may hold values from -0.25 to 0.25
- bias_one: float32 [1024], replicated, may hold values from -3 to 3
- weight_two: bfloat16 [1024, 1024], replicated, may hold values from -0.1875 to 0.1875
- bias_two: float32 [1024], replicated, may hold values from -3 to 3
- weight_three: bfloat16 [1024, 512], replicated, may hold values from -0.1875 to 0.1875
- bias_three: float32 [512], replicated, may hold values from -3 to 3
- weight_four: bfloat16 [512, 256], replicated, may hold values from -0.25 to 0.25
- bias_four: float32 [256], replicated, may hold values from -3 to 3
- weight_out: bfloat16 [256, 1], replicated, may hold values from -1 to 1
- bias_out: float32 [1], replicated, may hold values from -1.5 to 0
- bucket_index: int32 [16, 32768], P(None, ('gx', 'gy', 'gz')), may hold values from 0 to 4095
- labels: int32 [16, 32768], P(None, ('gx', 'gy', 'gz')), may hold values from 0 to 1
Outputs:
- bucket_stats: float32 [16, 4, 4096], P(None, None, 'gx')
- summary: float32 [16, 4], replicated
All inputs are finite; a program needn't handle non-finite values.
Results may differ from a plain program's by a relative error of at most 0.0045.
Values sent between devices are 32-bit elements; how exact they have to be, the bound alone decides.
No kernel may reach another device: no remote copies, remote signals or barrier semaphores. Data moves between devices by JAX's collectives and lax.ppermute only.
A program may use at most 128 MiB of HBM per device.

v0:
```python
import jax
import jax.numpy as jnp
from jax import lax
from jax.sharding import PartitionSpec as P

NBUCK = 4096


def split_up(value, dim, size):
    before, after = (value.shape[:dim], value.shape[dim + 1 :])
    return jnp.moveaxis(value.reshape(*before, size, -1, *after), dim, 0)


def sent_and_summed(value, axis, dim):
    tiles = split_up(value, dim, lax.axis_size(axis))
    arrived = lax.all_to_all(tiles, axis, split_axis=0, concat_axis=0, tiled=True)
    return arrived.sum(axis=0)


def gathered_total(value, axis):
    tiles = lax.all_gather(value, axis)
    return tiles.sum(axis=0)


def from_everyone(value, axis):
    size = lax.axis_size(axis)
    return lax.all_to_all(
        jnp.broadcast_to(value[None], (size, *value.shape)), axis, 0, 0, tiled=True
    )


def folded_in_pairs(pieces, combine):
    while len(jax.tree.leaves(pieces)[0]) > 1:
        pieces = jax.vmap(combine)(*(pieces[side::2] for side in (0, 1)))
    return pieces[0]


def carried_in(value, axis, combine, identity):
    size, index = (lax.axis_size(axis), lax.axis_index(axis))
    passed = jnp.arange(size) < index

    def kept(part, zero, own):
        part = jnp.where(
            passed.reshape(-1, *(1 for _ in own.shape)), part, jnp.asarray(zero, own.dtype)
        )
        return part

    pieces = from_everyone(value, axis)
    return folded_in_pairs(kept(pieces, identity, value), combine)


def one_axis_at_a_time(value, axes):
    for axis in axes:
        value = lax.psum(value, axis)
    return value


def joined_along(tiles, dim):
    shape = list(tiles.shape[1:])
    shape[dim] *= tiles.shape[0]
    return jnp.moveaxis(tiles, 0, dim).reshape(shape)


def gather_directly(value, axis, dim):
    tiles = from_everyone(value, axis)
    return joined_along(tiles, dim)


def layer_relu(inputs, weight, offset):
    return jax.nn.relu(jnp.dot(inputs, weight, preferred_element_type=jnp.float32) + offset).astype(
        jnp.bfloat16
    )


def bucket_reports(totals):
    positives = totals[:, 0]
    negatives = totals[:, 1]
    counts = jnp.maximum(positives + negatives, 1.0)
    return jnp.stack(
        [positives / counts, totals[:, 2] / counts, totals[:, 3] / counts, totals[:, 4] / counts],
        axis=1,
    )


def summarize(numerator, column_sums):
    pair_count = jnp.maximum(column_sums[:, 0] * column_sums[:, 1], 1.0)
    example_count = jnp.maximum(column_sums[:, 0] + column_sums[:, 1], 1.0)
    return jnp.stack(
        [
            numerator / pair_count,
            column_sums[:, 3] / example_count,
            column_sums[:, 2] / jnp.maximum(column_sums[:, 0], 1.0),
            column_sums[:, 4] / example_count,
        ],
        axis=1,
    )


def combine_add(earlier, later):
    return earlier + later


def split_parts(values):
    upper = values.astype(jnp.bfloat16)
    remain = values - upper.astype(jnp.float32)
    middle = remain.astype(jnp.bfloat16)
    lower = (remain - middle.astype(jnp.float32)).astype(jnp.bfloat16)
    return jnp.concatenate([upper, middle, lower], axis=0)


def merge_reports(histograms):
    bucket_share = sent_and_summed(histograms, ("gx", "gy"), 2)
    bucket_share = gathered_total(bucket_share, "gz")
    reports = bucket_reports(bucket_share)
    negatives = bucket_share[:, 1]
    negative_sums = jnp.sum(negatives, axis=1)
    before = carried_in(negative_sums, ("gx", "gy"), combine_add, jnp.zeros_like(negative_sums))
    below_count = before[:, None] + jnp.cumsum(negatives, axis=1) - negatives
    partial_numerator = jnp.sum(bucket_share[:, 0] * (below_count + 0.5 * negatives), axis=1)
    numerator, column_sums = (
        one_axis_at_a_time(partial_numerator, ("gx", "gy")),
        one_axis_at_a_time(jnp.sum(bucket_share, axis=2), ("gx", "gy")),
    )
    report_block = gather_directly(reports, "gy", 2)
    return (report_block, summarize(numerator, column_sums))


def on_device(
    interact,
    weight_one,
    bias_one,
    weight_two,
    bias_two,
    weight_three,
    bias_three,
    weight_four,
    bias_four,
    weight_out,
    bias_out,
    bucket_index,
    labels,
):
    intervals, local_rows, features_in = interact.shape
    flat_rows = interact.reshape(intervals * local_rows, features_in)
    hidden = layer_relu(flat_rows, weight_one, bias_one)
    hidden = layer_relu(hidden, weight_two, bias_two)
    hidden = layer_relu(hidden, weight_three, bias_three)
    hidden = layer_relu(hidden, weight_four, bias_four)
    logits = jnp.dot(hidden, weight_out, preferred_element_type=jnp.float32)[:, 0] + bias_out[0]
    logits = logits.reshape(intervals, local_rows)
    observed = labels.astype(jnp.float32)
    predicted = jax.nn.sigmoid(logits)
    losses = jax.nn.softplus(logits) - observed * logits
    squared = (predicted - observed) ** 2
    values = jnp.stack([observed, 1.0 - observed, predicted, losses, squared], axis=1)
    bucket_ids = lax.broadcasted_iota(jnp.int32, (1, NBUCK), 1)

    def histogram_one(inputs):
        row_values, buckets = inputs
        one_hot = (buckets[:, None] == bucket_ids).astype(jnp.bfloat16)
        parts = split_parts(row_values)
        partial_value = jnp.dot(parts, one_hot, preferred_element_type=jnp.float32)
        return jnp.sum(partial_value.reshape(3, row_values.shape[0], NBUCK), axis=0)

    histograms = lax.map(histogram_one, (values, bucket_index))
    bucket_stats, summary = merge_reports(histograms)
    return (bucket_stats, summary)


def solution(mesh):
    in_specs = (
        P(None, ("gx", "gy", "gz"), None),
        P(),
        P(),
        P(),
        P(),
        P(),
        P(),
        P(),
        P(),
        P(),
        P(),
        P(None, ("gx", "gy", "gz")),
        P(None, ("gx", "gy", "gz")),
    )
    out_specs = (P(None, None, "gx"), P())
    return jax.shard_map(
        on_device, mesh=mesh, in_specs=in_specs, out_specs=out_specs, check_vma=False
    )
```

profile of v0, /device:TPU:0, one launch (start us, length us, event | category | flops | bytes accessed | tf_op | source)
XLA Modules:
  0.0 154.5 jit_solution(18154456367741899383)
XLA Ops:
  1.4 0.8 copy-done
  2.3 18.6 %fusion.11 = f32[4096,1024]{1,0:T(8,128)} fusion(bf16[1024,1024]{1,0:T(8,128)(2,1)S(1)} %copy-done, f32[1024]{0:T(1024)} %param.17, bf16[4096,512]{1,0:T(8,128)(2,1)} %bitcast.83, bf16[512,1024]{1,0:T(8,128)(2,1)} %param.16), kind=kOutput, calls=%fused_computation.18 | convolution fusion | flops 12897484800 | bytes 24121344 | tf_op jit(solution)/shard_map/dot_general | solution.py:70
  20.9 10.5 %fusion.20 = bf16[4096,256]{1,0:T(8,128)(2,1)} fusion(bf16[512,256]{1,0:T(8,128)(2,1)S(1)} %copy-done.4, bf16[1024,512]{1,0:T(8,128)(2,1)S(1)} %copy-done.3, f32[4096,1024]{1,0:T(8,128)} %fusion.11, f32[1024]{0:T(1024)S(1)} %copy-done.5, f32[512]{0:T(512)S(1)} %copy-done.6, f32[256]{0:T(256)S(1)} %copy-done.7), kind=kOutput, calls=%fused_computation.28 | convolution fusion | flops 5390729216 | bytes 20192256 | tf_op jit(solution)/shard_map/dot_general | solution.py:70
  31.4 2.2 %fusion.34 = f32[1,4096]{1,0:T(1,128)S(1)} fusion(bf16[4096,256]{1,0:T(8,128)(2,1)} %fusion.20, bf16[256,1]{0,1:T(2,128)(2,1)S(1)} %copy-done.2), kind=kOutput, calls=%fused_computation.66 | convolution fusion | flops 2097152 | bytes 2114048 | tf_op jit(solution)/shard_map/dot_general | solution.py:149
  34.0 36.2 %while.11 = (s32[]{:T(128)}, f32[16,5,4096]{2,1,0:T(8,128)}, f32[16,5,256]{2,1,0:T(8,128)S(1)}, s32[16,256]{1,0:T(8,128)}, s32[]{:T(128)}, /*index=5*/f32[]{:T(128)}) while((s32[]{:T(128)}, f32[16,5,4096]{2,1,0:T(8,128)}, f32[16,5,256]{2,1,0:T(8,128)S(1)}, s32[16,256]{1,0:T(8,128)}, s32[]{:T(128)}, /*index=5*/f32[]{:T(128)}) %tuple.41), condition=%wide.region_2.3_spmd.clone, body=%wide.region_0.2_spmd.clone.sunk | while | flops 32577536 | bytes 1304657 | solution.py:165
  34.0 0.7 constant_dynamic-slice_fusion.2
  34.7 0.8 fusion.45
  36.3 0.7 constant_dynamic-slice_fusion.2
  37.0 0.8 fusion.45
  38.5 0.7 constant_dynamic-slice_fusion.2
  39.2 0.8 fusion.45
  40.8 0.7 constant_dynamic-slice_fusion.2
  41.5 0.8 fusion.45
  43.1 0.7 constant_dynamic-slice_fusion.2
  43.8 0.8 fusion.45
  45.3 0.7 constant_dynamic-slice_fusion.2
  46.0 0.8 fusion.45
  47.6 0.7 constant_dynamic-slice_fusion.2
  48.3 0.8 fusion.45
  49.8 0.7 constant_dynamic-slice_fusion.2
  50.5 0.8 fusion.45
  52.1 0.7 constant_dynamic-slice_fusion.2
  52.8 0.8 fusion.45
  54.4 0.7 constant_dynamic-slice_fusion.2
  55.1 0.8 fusion.45
  56.6 0.7 constant_dynamic-slice_fusion.2
  57.3 0.8 fusion.45
  58.9 0.7 constant_dynamic-slice_fusion.2
  59.6 0.8 fusion.45
  61.1 0.7 constant_dynamic-slice_fusion.2
  61.8 0.8 fusion.45
  64.1 0.8 fusion.45
  65.7 0.7 constant_dynamic-slice_fusion.2
  66.4 0.8 fusion.45
  67.9 0.7 constant_dynamic-slice_fusion.2
  68.6 0.8 fusion.45
  70.2 2.0 %reshape.100 = f32[16,5,16,256]{3,2,1,0:T(8,128)S(1)} reshape(f32[16,5,4096]{2,1,0:T(8,128)} %get-tuple-element.29) | data formatting | bytes 2621440 | tf_op jit(solution)/shard_map/reshape | solution.py:11
  72.2 1.8 %copy.54 = f32[16,16,5,256]{3,1,2,0:T(8,128)} copy(f32[16,16,5,256]{3,0,2,1:T(8,128)S(1)} %bitcast.76) | data formatting | bytes 2621440 | tf_op jit(solution)/shard_map/transpose | solution.py:11
  74.0 8.2 %all-to-all-start = ((f32[16,16,5,256]{3,1,2,0:T(8,128)}), f32[16,16,5,256]{3,1,2,0:T(8,128)S(1)}, u32[]{:S(2)}, u32[]{:S(2)}) async-start(f32[16,16,5,256]{3,1,2,0:T(8,128)} %copy.54), calls=%async_computation | async-start | bytes 2621440 | tf_op jit(solution)/shard_map/all_to_all | solution.py:16
  82.2 20.9 %all-to-all-done = f32[16,16,5,256]{3,1,2,0:T(8,128)S(1)} async-done(((f32[16,16,5,256]{3,1,2,0:T(8,128)}), f32[16,16,5,256]{3,1,2,0:T(8,128)S(1)}, u32[]{:S(2)}, u32[]{:S(2)}) %all-to-all-start) | async-done | bytes 1310752 | tf_op jit(solution)/shard_map/all_to_all | solution.py:16
  103.2 13.6 %all-gather = f32[128,5,256]{2,0,1:T(8,128)S(1)} all-gather(f32[16,5,256]{2,0,1:T(8,128)S(1)} %reduce_sum.54), channel_id=2, replica_groups=mesh['gx'=4,'gy'=4,'gz'=8] {'gz'}, dimensions={0}, use_global_device_ids=true | all-gather | bytes 737280 | tf_op jit(solution)/shard_map/all_gather | solution.py:21
  117.6 3.5 %all-to-all-start.2 = ((f32[16,1,16]{2,1,0:T(1,128)}), f32[16,1,16]{2,1,0:T(1,128)S(1)}, u32[]{:S(2)}, u32[]{:S(2)}) async-start(f32[16,1,16]{2,1,0:T(1,128)} %broadcast_in_dim.39), calls=%async_computation.2 | async-start | bytes 16384 | tf_op jit(solution)/shard_map/all_to_all | solution.py:27
  122.3 6.3 %all-to-all-done.2 = f32[16,1,16]{2,1,0:T(1,128)S(1)} async-done(((f32[16,1,16]{2,1,0:T(1,128)}), f32[16,1,16]{2,1,0:T(1,128)S(1)}, u32[]{:S(2)}, u32[]{:S(2)}) %all-to-all-start.2) | async-done | bytes 1056 | tf_op jit(solution)/shard_map/all_to_all | solution.py:27
  128.5 0.7 broadcast_in_dim.24
  129.3 3.4 %all-to-all-start.1 = ((f32[4,16,4,256]{3,2,1,0:T(4,128)}), f32[4,16,4,256]{3,2,1,0:T(4,128)S(1)}, u32[]{:S(2)}, u32[]{:S(2)}) async-start(f32[4,16,4,256]{3,2,1,0:T(4,128)} %broadcast_in_dim.24), calls=%async_computation.1 | async-start | bytes 524288 | tf_op jit(solution)/shard_map/all_to_all | solution.py:27
  133.1 9.0 %all-reduce.1 = (f32[16,5]{0,1:T(8,128)S(1)}, f32[16]{0:T(128)S(1)}) all-reduce(f32[16,5]{0,1:T(8,128)S(1)} %reduce_sum.58, f32[16]{0:T(128)S(1)} %fusion.28), channel_id=1, replica_groups=mesh['gx'=4,'gy'=4,'gz'=8] {'gx'}, use_global_device_ids=true, to_apply=%region_12.13 | all-reduce | flops 96 | bytes 768 | tf_op jit(solution)/shard_map/psum | solution.py:54
  142.1 11.0 %all-reduce = (f32[16,5]{0,1:T(8,128)S(1)}, f32[16]{0:T(128)S(1)}) all-reduce(f32[16,5]{0,1:T(8,128)S(1)} %get-tuple-element.54, f32[16]{0:T(128)S(1)} %get-tuple-element.55), channel_id=1, replica_groups=mesh['gx'=4,'gy'=4,'gz'=8] {'gy'}, use_global_device_ids=true, to_apply=%region_13.14 | all-reduce | flops 96 | bytes 768 | tf_op jit(solution)/shard_map/psum | solution.py:54
  153.8 0.7 copy.66
  (123 shorter events, 15.9 us)
Async XLA Ops:
  0.6 1.6 %copy-start = (bf16[1024,1024]{1,0:T(8,128)(2,1)S(1)}, bf16[1024,1024]{1,0:T(8,128)(2,1)}, u32[]{:S(2)}) copy-start(bf16[1024,1024]{1,0:T(8,128)(2,1)} %param.18) | copy-start | bytes 6291460
  2.2 18.6 %copy-start.3 = (bf16[1024,512]{1,0:T(8,128)(2,1)S(1)}, bf16[1024,512]{1,0:T(8,128)(2,1)}, u32[]{:S(2)}) copy-start(bf16[1024,512]{1,0:T(8,128)(2,1)} %param.20) | copy-start | bytes 3145732
  2.2 18.6 %copy-start.4 = (bf16[512,256]{1,0:T(8,128)(2,1)S(1)}, bf16[512,256]{1,0:T(8,128)(2,1)}, u32[]{:S(2)}) copy-start(bf16[512,256]{1,0:T(8,128)(2,1)} %param.22) | copy-start | bytes 786436
  2.2 18.6 %copy-start.5 = (f32[1024]{0:T(1024)S(1)}, f32[1024]{0:T(1024)}, u32[]{:S(2)}) copy-start(f32[1024]{0:T(1024)} %param.19) | copy-start | bytes 12292
  2.2 18.6 %copy-start.6 = (f32[512]{0:T(512)S(1)}, f32[512]{0:T(512)}, u32[]{:S(2)}) copy-start(f32[512]{0:T(512)} %param.21) | copy-start | bytes 6148
  2.3 18.6 %copy-start.7 = (f32[256]{0:T(256)S(1)}, f32[256]{0:T(256)}, u32[]{:S(2)}) copy-start(f32[256]{0:T(256)} %param.23) | copy-start | bytes 3076
  20.9 10.5 %copy-start.2 = (bf16[256,1]{0,1:T(2,128)(2,1)S(1)}, bf16[256,1]{0,1:T(2,128)(2,1)}, u32[]{:S(2)}) copy-start(bf16[256,1]{0,1:T(2,128)(2,1)} %param.24) | copy-start | bytes 1540
  20.9 12.8 %copy-start.1 = (s32[16,256]{1,0:T(8,128)S(1)}, s32[16,256]{1,0:T(8,128)}, u32[]{:S(2)}) copy-start(s32[16,256]{1,0:T(8,128)} %param.27) | copy-start | bytes 49156
  74.0 29.1 %all-to-all-start = ((f32[16,16,5,256]{3,1,2,0:T(8,128)}), f32[16,16,5,256]{3,1,2,0:T(8,128)S(1)}, u32[]{:S(2)}, u32[]{:S(2)}) async-start(f32[16,16,5,256]{3,1,2,0:T(8,128)} %copy.54), calls=%async_computation | async-start | bytes 2621440 | tf_op jit(solution)/shard_map/all_to_all | solution.py:16
  117.6 10.9 %all-to-all-start.2 = ((f32[16,1,16]{2,1,0:T(1,128)}), f32[16,1,16]{2,1,0:T(1,128)S(1)}, u32[]{:S(2)}, u32[]{:S(2)}) async-start(f32[16,1,16]{2,1,0:T(1,128)} %broadcast_in_dim.39), calls=%async_computation.2 | async-start | bytes 16384 | tf_op jit(solution)/shard_map/all_to_all | solution.py:27
  129.3 24.5 %all-to-all-start.1 = ((f32[4,16,4,256]{3,2,1,0:T(4,128)}), f32[4,16,4,256]{3,2,1,0:T(4,128)S(1)}, u32[]{:S(2)}, u32[]{:S(2)}) async-start(f32[4,16,4,256]{3,2,1,0:T(4,128)} %broadcast_in_dim.24), calls=%async_computation.1 | async-start | bytes 524288 | tf_op jit(solution)/shard_map/all_to_all | solution.py:27
where the time goes:
time: 156 us; the launch traced here: 154 us
  matrix products  44.1 us (28%)
  blocking collectives  33.6 us (22%)
  local copies, waits for them, and re-layouts  29.8 us (19%)
  waiting for transfers between devices  27.2 us (17%)
  starting transfers between devices  15 us (10%)
  other arithmetic  2.68 us (2%)
  between operations  1.7 us (1%)
    dot_general x2, matrix products, layer_relu(): jnp.dot(inputs, weight, preferred_element_type=jnp.float32) + offset  29.1 us
    all_to_all x1, waiting for transfers between devices, sent_and_summed(): lax.all_to_all(tiles, axis, split_axis=0, concat_axis=0, tiled=True)  20.9 us
    psum x2, blocking collectives, one_axis_at_a_time(): value = lax.psum(value, axis)  20 us
    all_gather x1, blocking collectives, gathered_total(): tiles = lax.all_gather(value, axis)  13.6 us
    dot_general x16, matrix products, histogram_one(): partial_value = jnp.dot(parts, one_hot, preferred_element_type=jnp.float32)  12.8 us
    dynamic_slice x16, local copies, waits for them, and re-layouts, on_device(): histograms = lax.map(histogram_one, (values, bucket_index))  11.2 us
    dynamic_update_slice x16, local copies, waits for them, and re-layouts, on_device(): histograms = lax.map(histogram_one, (values, bucket_index))  10.6 us
    all_to_all x1, starting transfers between devices, sent_and_summed(): lax.all_to_all(tiles, axis, split_axis=0, concat_axis=0, tiled=True)  8.16 us
  transfers between devices with their start and end apart: 3, of which 2 were waited for; matrix products, arithmetic and copies ran while one was open for 1% of the time, Pallas kernels for 0%

commit v1 on v0

--- a/solution.py
+++ b/solution.py
@@ -4,6 +4,11 @@
 from jax.sharding import PartitionSpec as P
 
 NBUCK = 4096
+
+
+def render_strips_all_for(my_data, peer_axis):
+    clean = jnp.sum(jax.lax.all_gather(my_data, peer_axis), 0)
+    return clean
 
 
 def split_up(value, dim, size):
@@ -51,7 +56,7 @@
 
 def one_axis_at_a_time(value, axes):
     for axis in axes:
-        value = lax.psum(value, axis)
+        value = render_strips_all_for(value, peer_axis=axis)
     return value
 
 

time: 156 us -> 177 us (1.13)
  blocking collectives: 33.6 us -> 59.6 us
  waiting for transfers between devices: 27.2 us -> 18.4 us
  local copies, waits for them, and re-layouts: 29.8 us -> 31.7 us
    all_gather x0 -> x2, blocking collectives: none -> 25 us  [render_strips_all_for(): clean = jnp.sum(jax.lax.all_gather(my_data, peer_axis), 0)]
    unnamed x0 -> x2, blocking collectives: none -> 21 us
    psum x2 -> x0, blocking collectives: 20 us -> none  [one_axis_at_a_time(): value = lax.psum(value, axis)]
    all_to_all x2, waiting for transfers between devices: 6.27 us -> 0.01 us  [from_everyone(): lax.all_to_all(jnp.broadcast_to(value[None], (size, *value.shape)), axis,...]
    all_to_all x1, waiting for transfers between devices: 20.9 us -> 18.4 us  [sent_and_summed(): lax.all_to_all(tiles, axis, split_axis=0, concat_axis=0, tiled=True)]
  transfers between devices with their start and end apart: 3 -> 3, of which waited for: 2 -> 1; matrix products, arithmetic and copies ran while one was open for 1% -> 2% of each run, Pallas kernels for 0% -> 0%
where the time goes in v1:
time: 177 us; the launch traced here: 175 us
  blocking collectives  59.6 us (34%)
  matrix products  44.1 us (25%)
  local copies, waits for them, and re-layouts  31.7 us (18%)
  waiting for transfers between devices  18.4 us (10%)
  starting transfers between devices  15.3 us (9%)
  between operations  3 us (2%)
  other arithmetic  2.75 us (2%)
    dot_general x2, matrix products, layer_relu(): jnp.dot(inputs, weight, preferred_element_type=jnp.float32) + offset  29.1 us
    all_gather x2, blocking collectives, render_strips_all_for(): clean = jnp.sum(jax.lax.all_gather(my_data, peer_axis), 0)  25 us
    unnamed x2, blocking collectives  21 us
    all_to_all x1, waiting for transfers between devices, sent_and_summed(): lax.all_to_all(tiles, axis, split_axis=0, concat_axis=0, tiled=True)  18.4 us
    all_gather x1, blocking collectives, gathered_total(): tiles = lax.all_gather(value, axis)  13.6 us
    dot_general x16, matrix products, histogram_one(): partial_value = jnp.dot(parts, one_hot, preferred_element_type=jnp.float32)  12.8 us
    dynamic_slice x16, local copies, waits for them, and re-layouts, on_device(): histograms = lax.map(histogram_one, (values, bucket_index))  11.2 us
    dynamic_update_slice x16, local copies, waits for them, and re-layouts, on_device(): histograms = lax.map(histogram_one, (values, bucket_index))  10.6 us
  transfers between devices with their start and end apart: 3, of which 1 were waited for; matrix products, arithmetic and copies ran while one was open for 2% of the time, Pallas kernels for 0%

profile of v1, /device:TPU:0, one launch (start us, length us, event | category | flops | bytes accessed | tf_op | source)
XLA Modules:
  0.0 175.2 jit_solution(15671276114538975145)
XLA Ops:
  1.4 0.8 copy-done
  2.3 18.6 %fusion.11 = f32[4096,1024]{1,0:T(8,128)} fusion(bf16[1024,1024]{1,0:T(8,128)(2,1)S(1)} %copy-done, f32[1024]{0:T(1024)} %param.17, bf16[4096,512]{1,0:T(8,128)(2,1)} %bitcast.85, bf16[512,1024]{1,0:T(8,128)(2,1)} %param.16), kind=kOutput, calls=%fused_computation.18 | convolution fusion | flops 12897484800 | bytes 24121344 | tf_op jit(solution)/shard_map/dot_general | solution.py:75
  20.9 10.5 %fusion.20 = bf16[4096,256]{1,0:T(8,128)(2,1)} fusion(bf16[512,256]{1,0:T(8,128)(2,1)S(1)} %copy-done.4, bf16[1024,512]{1,0:T(8,128)(2,1)S(1)} %copy-done.3, f32[4096,1024]{1,0:T(8,128)} %fusion.11, f32[1024]{0:T(1024)S(1)} %copy-done.5, f32[512]{0:T(512)S(1)} %copy-done.6, f32[256]{0:T(256)S(1)} %copy-done.7), kind=kOutput, calls=%fused_computation.28 | convolution fusion | flops 5390729216 | bytes 20192256 | tf_op jit(solution)/shard_map/dot_general | solution.py:75
  31.4 2.2 %fusion.33 = f32[1,4096]{1,0:T(1,128)S(1)} fusion(bf16[4096,256]{1,0:T(8,128)(2,1)} %fusion.20, bf16[256,1]{0,1:T(2,128)(2,1)S(1)} %copy-done.2), kind=kOutput, calls=%fused_computation.65 | convolution fusion | flops 2097152 | bytes 2114048 | tf_op jit(solution)/shard_map/dot_general | solution.py:154
  34.0 36.2 %while.11 = (s32[]{:T(128)}, f32[16,5,4096]{2,1,0:T(8,128)}, f32[16,5,256]{2,1,0:T(8,128)S(1)}, s32[16,256]{1,0:T(8,128)}, s32[]{:T(128)}, /*index=5*/f32[]{:T(128)}) while((s32[]{:T(128)}, f32[16,5,4096]{2,1,0:T(8,128)}, f32[16,5,256]{2,1,0:T(8,128)S(1)}, s32[16,256]{1,0:T(8,128)}, s32[]{:T(128)}, /*index=5*/f32[]{:T(128)}) %tuple.42), condition=%wide.region_2.3_spmd.clone, body=%wide.region_0.2_spmd.clone.sunk | while | flops 32577536 | bytes 1304657 | solution.py:170
  34.0 0.7 constant_dynamic-slice_fusion.2
  34.7 0.8 fusion.44
  36.3 0.7 constant_dynamic-slice_fusion.2
  37.0 0.8 fusion.44
  38.5 0.7 constant_dynamic-slice_fusion.2
  39.2 0.8 fusion.44
  40.8 0.7 constant_dynamic-slice_fusion.2
  41.5 0.8 fusion.44
  43.1 0.7 constant_dynamic-slice_fusion.2
  43.8 0.8 fusion.44
  45.3 0.7 constant_dynamic-slice_fusion.2
  46.0 0.8 fusion.44
  47.6 0.7 constant_dynamic-slice_fusion.2
  48.3 0.8 fusion.44
  49.8 0.7 constant_dynamic-slice_fusion.2
  50.5 0.8 fusion.44
  52.1 0.7 constant_dynamic-slice_fusion.2
  52.8 0.8 fusion.44
  54.4 0.7 constant_dynamic-slice_fusion.2
  55.1 0.8 fusion.44
  56.6 0.7 constant_dynamic-slice_fusion.2
  57.3 0.8 fusion.44
  58.9 0.7 constant_dynamic-slice_fusion.2
  59.6 0.8 fusion.44
  61.9 0.8 fusion.44
  63.4 0.7 constant_dynamic-slice_fusion.2
  64.1 0.8 fusion.44
  66.4 0.8 fusion.44
  67.9 0.7 constant_dynamic-slice_fusion.2
  68.6 0.8 fusion.44
  70.2 2.1 %reshape.118 = f32[16,5,16,256]{3,2,1,0:T(8,128)S(1)} reshape(f32[16,5,4096]{2,1,0:T(8,128)} %get-tuple-element.29) | data formatting | bytes 2621440 | tf_op jit(solution)/shard_map/reshape | solution.py:16
  72.2 1.8 %copy.54 = f32[16,16,5,256]{3,1,2,0:T(8,128)} copy(f32[16,16,5,256]{3,0,2,1:T(8,128)S(1)} %bitcast.76) | data formatting | bytes 2621440 | tf_op jit(solution)/shard_map/transpose | solution.py:16
  74.1 8.2 %all-to-all-start = ((f32[16,16,5,256]{3,1,2,0:T(8,128)}), f32[16,16,5,256]{3,1,2,0:T(8,128)S(1)}, u32[]{:S(2)}, u32[]{:S(2)}) async-start(f32[16,16,5,256]{3,1,2,0:T(8,128)} %copy.54), calls=%async_computation | async-start | bytes 2621440 | tf_op jit(solution)/shard_map/all_to_all | solution.py:21
  84.8 18.4 %all-to-all-done = f32[16,16,5,256]{3,1,2,0:T(8,128)S(1)} async-done(((f32[16,16,5,256]{3,1,2,0:T(8,128)}), f32[16,16,5,256]{3,1,2,0:T(8,128)S(1)}, u32[]{:S(2)}, u32[]{:S(2)}) %all-to-all-start) | async-done | bytes 1310752 | tf_op jit(solution)/shard_map/all_to_all | solution.py:21
  103.3 13.6 %all-gather = f32[128,5,256]{2,0,1:T(8,128)S(1)} all-gather(f32[16,5,256]{2,0,1:T(8,128)S(1)} %reduce_sum.92), channel_id=2, replica_groups=mesh['gx'=4,'gy'=4,'gz'=8] {'gz'}, dimensions={0}, use_global_device_ids=true | all-gather | bytes 737280 | tf_op jit(solution)/shard_map/all_gather | solution.py:26
  117.6 3.5 %all-to-all-start.2 = ((f32[16,1,16]{2,1,0:T(1,128)}), f32[16,1,16]{2,1,0:T(1,128)S(1)}, u32[]{:S(2)}, u32[]{:S(2)}) async-start(f32[16,1,16]{2,1,0:T(1,128)} %broadcast_in_dim.39), calls=%async_computation.2 | async-start | bytes 16384 | tf_op jit(solution)/shard_map/all_to_all | solution.py:32
  122.3 12.7 %all-gather.5 = f32[4,16,5]{1,2,0:T(8,128)S(1)} all-gather(f32[1,16,5]{1,2,0:T(8,128)S(1)} %bitcast.83), channel_id=5, replica_groups=mesh['gx'=4,'gy'=4,'gz'=8] {'gx'}, dimensions={0}, use_global_device_ids=true | all-gather | bytes 1600 | tf_op jit(solution)/shard_map/all_gather | solution.py:10
  135.0 12.3 %all-gather.6 = f32[4,16,5]{1,2,0:T(8,128)S(1)} all-gather(f32[1,16,5]{1,2,0:T(8,128)S(1)} %bitcast.84), channel_id=6, replica_groups=mesh['gx'=4,'gy'=4,'gz'=8] {'gy'}, dimensions={0}, use_global_device_ids=true | all-gather | bytes 1600 | tf_op jit(solution)/shard_map/all_gather | solution.py:10
  147.3 0.7 broadcast_in_dim.24
  148.1 3.6 %all-to-all-start.1 = ((f32[4,16,4,256]{3,2,1,0:T(4,128)}), f32[4,16,4,256]{3,2,1,0:T(4,128)S(1)}, u32[]{:S(2)}, u32[]{:S(2)}) async-start(f32[4,16,4,256]{3,2,1,0:T(4,128)} %broadcast_in_dim.24), calls=%async_computation.1 | async-start | bytes 524288 | tf_op jit(solution)/shard_map/all_to_all | solution.py:32
  152.4 10.1 %all-reduce = f32[64]{0:T(128)S(1)} all-reduce(f32[64]{0:T(128)S(1)} %dynamic-update-slice), channel_id=3, replica_groups=mesh['gx'=4,'gy'=4,'gz'=8] {'gx'}, use_global_device_ids=true, to_apply=%add | all-reduce | flops 64 | bytes 512
  162.8 10.9 %all-reduce.1 = f32[64]{0:T(128)S(1)} all-reduce(f32[64]{0:T(128)S(1)} %dynamic-update-slice.1), channel_id=4, replica_groups=mesh['gx'=4,'gy'=4,'gz'=8] {'gy'}, use_global_device_ids=true, to_apply=%add.1 | all-reduce | flops 64 | bytes 512
  174.5 0.7 copy.66
  (140 shorter events, 18.5 us)
Async XLA Ops:
  0.6 1.6 copy-start
  2.2 18.6 %copy-start.3 = (bf16[1024,512]{1,0:T(8,128)(2,1)S(1)}, bf16[1024,512]{1,0:T(8,128)(2,1)}, u32[]{:S(2)}) copy-start(bf16[1024,512]{1,0:T(8,128)(2,1)} %param.20) | copy-start | bytes 3145732
  2.2 18.6 %copy-start.4 = (bf16[512,256]{1,0:T(8,128)(2,1)S(1)}, bf16[512,256]{1,0:T(8,128)(2,1)}, u32[]{:S(2)}) copy-start(bf16[512,256]{1,0:T(8,128)(2,1)} %param.22) | copy-start | bytes 786436
  2.2 18.6 %copy-start.5 = (f32[1024]{0:T(1024)S(1)}, f32[1024]{0:T(1024)}, u32[]{:S(2)}) copy-start(f32[1024]{0:T(1024)} %param.19) | copy-start | bytes 12292
  2.2 18.6 %copy-start.6 = (f32[512]{0:T(512)S(1)}, f32[512]{0:T(512)}, u32[]{:S(2)}) copy-start(f32[512]{0:T(512)} %param.21) | copy-start | bytes 6148
  2.3 18.6 %copy-start.7 = (f32[256]{0:T(256)S(1)}, f32[256]{0:T(256)}, u32[]{:S(2)}) copy-start(f32[256]{0:T(256)} %param.23) | copy-start | bytes 3076
  20.9 10.5 %copy-start.2 = (bf16[256,1]{0,1:T(2,128)(2,1)S(1)}, bf16[256,1]{0,1:T(2,128)(2,1)}, u32[]{:S(2)}) copy-start(bf16[256,1]{0,1:T(2,128)(2,1)} %param.24) | copy-start | bytes 1540
  20.9 12.8 %copy-start.1 = (s32[16,256]{1,0:T(8,128)S(1)}, s32[16,256]{1,0:T(8,128)}, u32[]{:S(2)}) copy-start(s32[16,256]{1,0:T(8,128)} %param.27) | copy-start | bytes 49156
  70.2 12.1 %copy-start.9 = (u32[128]{0:T(128)S(1)}, u32[128]{0:T(128)}, u32[]{:S(2)}) copy-start(u32[128]{0:T(128)} %constant.49) | copy-start | bytes 1540
  70.2 12.7 %copy-start.8 = (u32[128]{0:T(128)S(1)}, u32[128]{0:T(128)}, u32[]{:S(2)}) copy-start(u32[128]{0:T(128)} %constant.54) | copy-start | bytes 1540
  74.1 29.1 %all-to-all-start = ((f32[16,16,5,256]{3,1,2,0:T(8,128)}), f32[16,16,5,256]{3,1,2,0:T(8,128)S(1)}, u32[]{:S(2)}, u32[]{:S(2)}) async-start(f32[16,16,5,256]{3,1,2,0:T(8,128)} %copy.54), calls=%async_computation | async-start | bytes 2621440 | tf_op jit(solution)/shard_map/all_to_all | solution.py:21
  117.6 29.7 %all-to-all-start.2 = ((f32[16,1,16]{2,1,0:T(1,128)}), f32[16,1,16]{2,1,0:T(1,128)S(1)}, u32[]{:S(2)}, u32[]{:S(2)}) async-start(f32[16,1,16]{2,1,0:T(1,128)} %broadcast_in_dim.39), calls=%async_computation.2 | async-start | bytes 16384 | tf_op jit(solution)/shard_map/all_to_all | solution.py:32
  148.1 26.4 %all-to-all-start.1 = ((f32[4,16,4,256]{3,2,1,0:T(4,128)}), f32[4,16,4,256]{3,2,1,0:T(4,128)S(1)}, u32[]{:S(2)}, u32[]{:S(2)}) async-start(f32[4,16,4,256]{3,2,1,0:T(4,128)} %broadcast_in_dim.24), calls=%async_computation.1 | async-start | bytes 524288 | tf_op jit(solution)/shard_map/all_to_all | solution.py:32
